TPU v7x, 32 devices: a whole 2x2x4 slice. The times are simulated.
32 devices in a mesh: blk: 16 (over z, y, x), band: 2 (over core).
Axes of the slice: x: 2, y: 2, z: 4, core: 2. Of those that a mesh axis runs over, the one named last changes fastest.
Arguments:
- disp_fwd: float32 [16, 2, 25, 2048], P('blk', 'band'), may hold values from -6 to 6
- prev_fwd: float32 [16, 2, 25, 2048], P('blk', 'band'), may hold values from -6 to 6
- disp_adj: float32 [16, 2, 25, 2048], P('blk', 'band'), may hold values from -6 to 6
- prev_adj: float32 [16, 2, 25, 2048], P('blk', 'band'), may hold values from -6 to 6
- modulus: float32 [16, 2, 25, 2048], P('blk', 'band'), may hold values from 0.5 to 2
- radius: float32 [16, 2, 25], P('blk', 'band'), may hold values from 256 to 2048
- step_scale: float32 [16, 2, 25], P('blk', 'band'), may hold values from 0.01 to 0.04
- kernel_in: float32 [16, 2, 25, 2048], P('blk', 'band'), may hold values from -6 to 6
- buckets: int32 [16, 2], P('blk', 'band'), may hold values from 0 to 3
- halo_count: int32 [16, 2, 4], P('blk', 'band'), may hold values from 0 to 8, as said below
- blk_nodes: int32 [16, 2, 2, 8], P('blk', 'band'), may hold values from 0 to 24, as said below
- band_nodes: int32 [16, 2, 2, 4], P('blk', 'band'), may hold values from 0 to 24, as said below
Outputs:
- next_fwd: float32 [16, 2, 25, 2048], P('blk', 'band')
- next_adj: float32 [16, 2, 25, 2048], P('blk', 'band')
- kernel_out: float32 [16, 2, 25, 2048], P('blk', 'band')
Inputs may be any that keep to these rules, and one draw needn't show every extreme that they name: `halo_count`: entries 0 and 1 count the nodes shared with the blk neighbour below and above, entries 2 and 3 with the band neighbour below and above. A device's count toward a neighbour equals the neighbour's count back; counts toward the outside of the grid are zero; some pair along blk shares 8 nodes and some pair along band 4. Slot k of a device's list toward a blk neighbour and slot k of that neighbour's list back hold copies of one node; slots at or past the count are unused. The 24 ids of one device over blk_nodes and band_nodes are all different. `band_nodes`: slot k of a device's list toward a band neighbour and slot k of that neighbour's list back hold copies of one node; slots at or past the count are unused; ids are different from those of blk_nodes on the same device.
All inputs are finite; a program needn't handle non-finite values.
Results may differ from a plain program's by a relative error of at most 0.0046.
Values sent between devices are 32-bit elements; how exact they have to be, the bound alone decides.
A program may use at most 64 MiB of HBM per device.

v0:
```python
import functools
import math

import jax
import jax.numpy as jnp
import ml_dtypes
import numpy as np
from jax import lax
from jax.experimental import pallas as pl
from jax.experimental.pallas import tpu as pltpu
from jax.sharding import PartitionSpec as P

MESH = pl.DeviceIdType.MESH


def gll_tables():
    inner_root = math.sqrt(3.0 / 7.0)
    points = np.array([-1.0, -inner_root, 0.0, inner_root, 1.0])
    weights = np.array([0.1, 49.0 / 90.0, 32.0 / 45.0, 49.0 / 90.0, 0.1])
    legendre = (35.0 * points**4 - 30.0 * points**2 + 3.0) / 8.0
    derivative = np.zeros((5, 5))
    for target in range(5):
        for source in range(5):
            if target != source:
                derivative[target, source] = (
                    legendre[target] / legendre[source] / (points[target] - points[source])
                )
    derivative[0, 0] = -5.0
    derivative[4, 4] = 5.0
    return derivative.astype(np.float32), np.outer(weights, weights).astype(np.float32)


def half_table(mode_total, width):
    sample_len = 2 * mode_total
    rows = np.arange(2 * mode_total, dtype=np.int64)
    quarter = (rows >= mode_total) * (sample_len // 4)
    phase = ((rows % mode_total)[:, None] * np.arange(mode_total)[None] + quarter[:, None]) % sample_len
    levels = np.cos(np.arange(sample_len) * (2.0 * math.pi / sample_len)) * math.sqrt(2.0 / sample_len)
    levels = levels.astype(np.float32).astype(ml_dtypes.bfloat16)
    table = levels[phase]
    return table.reshape(2 * mode_total, mode_total // width, width).transpose(1, 0, 2)


def split_bf16(value):
    high = value.astype(np.float32).astype(ml_dtypes.bfloat16)
    low = (value.astype(np.float32) - high.astype(np.float32)).astype(ml_dtypes.bfloat16)
    return high, low


def node_operators(pad):
    derivative, quadrature = gll_tables()
    eye = np.eye(5, dtype=np.float32)
    along_s = np.zeros((pad, pad), np.float32)
    along_z = np.zeros((pad, pad), np.float32)
    along_s[:25, :25] = np.kron(derivative, eye)
    along_z[:25, :25] = np.kron(eye, derivative)
    grad_hi, grad_lo = split_bf16(np.concatenate([along_s, along_z], axis=0))
    div_hi, div_lo = split_bf16(np.concatenate([along_s.T, along_z.T], axis=1))
    quad = np.zeros((pad, 128), np.float32)
    quad[:25] = quadrature.reshape(25, 1)
    return (
        np.concatenate([grad_hi, grad_hi, grad_lo], axis=1),
        np.concatenate([div_hi, div_hi, div_lo], axis=1),
        quad,
    )


def halves(value):
    high = value.astype(jnp.bfloat16)
    low = (value - high.astype(jnp.float32)).astype(jnp.bfloat16)
    return high, low


def mm(lhs, rhs):
    return jnp.dot(lhs, rhs, preferred_element_type=jnp.float32)


def padded(value, pad):
    extra = pad - value.shape[0]
    return jnp.concatenate([value, jnp.zeros((extra, value.shape[1]), value.dtype)], axis=0)


def take(ref, nodes, start, size):
    stride = ref.shape[0] // nodes
    return jnp.concatenate(
        [ref[pl.ds(start // 128 + j, nodes, stride=stride), :] for j in range(size // 128)], axis=1
    )


def put(ref, nodes, start, value):
    stride = ref.shape[0] // nodes
    for j in range(value.shape[1] // 128):
        ref[pl.ds(start // 128 + j, nodes, stride=stride), :] = value[:, j * 128 : (j + 1) * 128]


def column_of(row, pad):
    count = row.shape[1]
    sub = lax.broadcasted_iota(jnp.int32, (pad, count), 0)
    lane = lax.broadcasted_iota(jnp.int32, (pad, count), 1)
    return jnp.sum(jnp.where(sub == lane, row, 0.0), axis=1, keepdims=True)


def kernel(
    blk_total,
    band_total,
    nodes,
    pad,
    width,
    disp_fwd_hbm,
    prev_fwd_hbm,
    disp_adj_hbm,
    prev_adj_hbm,
    modulus_hbm,
    kernel_in_hbm,
    radius_hbm,
    step_hbm,
    bucket_hbm,
    grad_hbm,
    div_hbm,
    quad_hbm,
    counts_hbm,
    blk_nodes_hbm,
    band_nodes_hbm,
    table_hbm,
    next_fwd,
    next_adj,
    kernel_out,
    held,
    radius,
    step_scale,
    bucket,
    grad_op,
    div_op,
    quad,
    counts,
    blk_nodes,
    band_nodes,
    table,
    rows,
    low,
    stiff,
    send_blk,
    send_band,
    recv_blk,
    recv_band,
    held_sem,
    small_sem,
    table_sem,
    send_sem,
    recv_sem,
):
    disp_fwd, disp_adj, modulus, kernel_in, prev_fwd, prev_adj = (held.at[i] for i in range(6))
    sources = (disp_fwd_hbm, disp_adj_hbm, modulus_hbm, kernel_in_hbm, prev_fwd_hbm, prev_adj_hbm)
    fetches = [
        pltpu.make_async_copy(source, held.at[i], held_sem.at[i])
        for i, source in enumerate(sources)
    ]
    small = [
        pltpu.make_async_copy(source, target, small_sem.at[i])
        for i, (source, target) in enumerate(
            (
                (radius_hbm, radius),
                (step_hbm, step_scale),
                (bucket_hbm, bucket),
                (grad_hbm, grad_op),
                (div_hbm, div_op),
                (quad_hbm, quad),
                (counts_hbm, counts),
                (blk_nodes_hbm, blk_nodes),
                (band_nodes_hbm, band_nodes),
            )
        )
    ]
    fetches[0].start()
    for copy in small:
        copy.start()
    fetches[1].start()
    blk = lax.axis_index("blk")
    band = lax.axis_index("band")
    half = disp_fwd_hbm.shape[0] // nodes * 128 // 2
    chunks = half // width
    blk_slots = blk_nodes.shape[-1]
    band_slots = band_nodes.shape[-1]
    links = [
        (blk > 0, (blk - 1, band)),
        (blk < blk_total - 1, (blk + 1, band)),
        (band > 0, (blk, band - 1)),
        (band < band_total - 1, (blk, band + 1)),
    ]
    loads = [
        pltpu.make_async_copy(table_hbm.at[c], table.at[c], table_sem.at[c]) for c in range(chunks)
    ]
    for load in loads:
        load.start()
    for fetch in fetches[2:]:
        fetch.start()
    barrier = pltpu.get_barrier_semaphore()
    for here, peer in links:

        @pl.when(here)
        def _():
            pl.semaphore_signal(barrier, inc=1, device_id=peer, device_id_type=MESH)

    def landing(c, side):
        return recv_blk.at[c, side] if side < 2 else recv_band.at[c, side - 2]

    def leaving(c, side):
        return send_blk.at[c, side] if side < 2 else send_band.at[c, side - 2]

    def transfer(c, side):
        return pltpu.make_async_remote_copy(
            src_ref=leaving(c, side),
            dst_ref=landing(c, side ^ 1),
            send_sem=send_sem.at[c, side],
            recv_sem=recv_sem.at[c, side ^ 1],
            device_id=links[side][1],
            device_id_type=MESH,
        )

    def arrival(c, side):
        return pltpu.make_async_remote_copy(
            src_ref=leaving(c, side),
            dst_ref=landing(c, side),
            send_sem=send_sem.at[c, side],
            recv_sem=recv_sem.at[c, side],
            device_id=links[side][1],
            device_id_type=MESH,
        )

    for side in range(4):

        @pl.when(jnp.logical_not(links[side][0]))
        def _():
            for c in range(chunks):
                ref = landing(c, side)
                ref[...] = jnp.zeros(ref.shape, ref.dtype)

    for copy in small:
        copy.wait()
    level = bucket[...]
    tops = [max(half // 64, 1), max(half // 16, 1), max(half // 4, 1), half]
    limit = jnp.where(
        level == 0, tops[0], jnp.where(level == 1, tops[1], jnp.where(level == 2, tops[2], tops[3]))
    )
    radius_col = column_of(radius[0], pad)
    sub_col = lax.broadcasted_iota(jnp.int32, (pad, 1), 0)
    inv_radius = jnp.where(sub_col < nodes, 1.0 / radius_col, 0.0)
    growth = column_of(step_scale[0], pad)
    quad_col = quad[:, 0:1]
    fields = ((disp_fwd, prev_fwd, next_fwd), (disp_adj, prev_adj, next_adj))

    def orders(c):
        m = lax.broadcasted_iota(jnp.int32, (1, width), 1) + c * width
        kept = (m < limit).astype(jnp.float32)
        sign = (1 - 2 * (m % 2)).astype(jnp.float32)
        return m.astype(jnp.float32), kept, sign

    for f, (disp, _, _) in enumerate(fields):
        fetches[f].wait()
        for c in range(chunks):
            m, kept, sign = orders(c)
            re_cols = slice(c * width, (c + 1) * width)
            im_cols = slice(half + c * width, half + (c + 1) * width)
            real = padded(take(disp, nodes, c * width, width), pad) * kept
            imag = padded(take(disp, nodes, half + c * width, width), pad) * kept
            spin_re = -m * imag * inv_radius
            spin_im = m * real * inv_radius
            for k, (re_part, im_part) in enumerate(((real, imag), (spin_re, spin_im))):
                at = (4 * f + 2 * k) * pad
                rows[at : at + pad, re_cols] = re_part.astype(jnp.bfloat16)
                rows[at : at + pad, im_cols] = im_part.astype(jnp.bfloat16)
                rows[at + pad : at + 2 * pad, re_cols] = (re_part * sign).astype(jnp.bfloat16)
                rows[at + pad : at + 2 * pad, im_cols] = (im_part * sign).astype(jnp.bfloat16)

    for c in range(chunks):
        loads[c].wait()
        if c == 0:
            fetches[2].wait()
            fetches[3].wait()
        samples = mm(rows[...], table[c])
        chunk_cols = slice(c * width, (c + 1) * width)
        for h in range(2):
            start = h * half + c * width
            weight = padded(take(modulus, nodes, start, width), pad) * quad_col
            terms = []
            for f in range(2):
                at = (4 * f + h) * pad
                physical = samples[at : at + pad]
                azimuthal = samples[at + 2 * pad : at + 3 * pad]
                high, lower = halves(physical)
                grads = mm(grad_op[...], jnp.concatenate([high, lower, high], axis=0))
                grad_s, grad_z = grads[:pad], grads[pad:]
                high_s, low_s = halves(weight * grad_s)
                high_z, low_z = halves(weight * grad_z)
                diverge = mm(
                    div_op[...],
                    jnp.concatenate([high_s, high_z, low_s, low_z, high_s, high_z], axis=0),
                )
                low[at : at + pad, chunk_cols] = diverge.astype(jnp.bfloat16)
                low[at + 2 * pad : at + 3 * pad, chunk_cols] = (weight * azimuthal).astype(
                    jnp.bfloat16
                )
                terms.append((grad_s, grad_z, azimuthal))
            product = sum(one * two for one, two in zip(*terms))
            change = (quad_col * product)[:nodes]
            put(kernel_out, nodes, start, take(kernel_in, nodes, start, width) - change)

    pl.semaphore_wait(barrier, sum(here.astype(jnp.int32) for here, _ in links))

    for c in range(chunks):
        m, kept, sign = orders(c)
        cosines = mm(low[...], table[c, :half])
        sines = mm(low[...], table[c, half:])

        def joined(result, group):
            at = group * pad
            return result[at : at + pad] + sign * result[at + pad : at + 2 * pad]

        for f in range(2):
            real = kept * (joined(cosines, 4 * f) + m * joined(sines, 4 * f + 2) * inv_radius)
            imag = kept * (joined(sines, 4 * f) - m * joined(cosines, 4 * f + 2) * inv_radius)
            stiff[c, f, :, :width] = real
            stiff[c, f, :, width:] = imag
        for side in range(2):
            for f in range(2):
                for s in range(blk_slots):
                    node = blk_nodes[0, 0, side, s]
                    at = f * blk_slots + s
                    send_blk[c, side, at : at + 1, :] = stiff[c, f, pl.ds(node, 1), :]
                for s in range(band_slots):
                    node = band_nodes[0, 0, side, s]
                    at = f * band_slots + s
                    send_band[c, side, at : at + 1, :] = stiff[c, f, pl.ds(node, 1), :]
        for side in range(4):

            @pl.when(links[side][0])
            def _():
                transfer(c, side).start()

    slot_rows = 4 * (blk_slots + band_slots)
    lane = lax.broadcasted_iota(jnp.int32, (1, 2 * slot_rows), 1) % slot_rows
    target = jnp.full((1, 2 * slot_rows), -1, jnp.int32)
    at = 0
    for side in range(4):
        lists = blk_nodes if side < 2 else band_nodes
        for f in range(2):
            for s in range(lists.shape[-1]):
                node = jnp.where(s < counts[0, 0, side], lists[0, 0, side % 2, s] + f * pad, -1)
                target = jnp.where(lane == at, node, target)
                at += 1
    sub = lax.broadcasted_iota(jnp.int32, (2 * pad, 2 * slot_rows), 0)
    placer = jnp.where(sub == target, 1.0, 0.0).astype(jnp.bfloat16)

    fetches[4].wait()
    fetches[5].wait()
    for c in range(chunks):
        for side in range(4):

            @pl.when(links[side][0])
            def _():
                arrival(c, side).wait_recv()

        m, kept, _ = orders(c)
        arrived = jnp.concatenate([landing(c, side)[...] for side in range(4)], axis=0)
        high, lower = halves(arrived)
        placed = mm(placer, jnp.concatenate([high, lower], axis=0))
        for f, (disp, prev, out) in enumerate(fields):
            for part in range(2):
                start = part * half + c * width
                now, before = (take(ref, nodes, start, width) for ref in (disp, prev))
                sect = slice(part * width, (part + 1) * width)
                total = stiff[c, f, :, sect] + placed[f * pad : (f + 1) * pad, sect]
                put(out, nodes, start, kept * (2.0 * now - before - (growth * total)[:nodes]))
    for c in range(chunks):
        for side in range(4):

            @pl.when(links[side][0])
            def _():
                transfer(c, side).wait_send()


def deliver(one, two, three, one_out, two_out, three_out, sems):
    copies = [
        pltpu.make_async_copy(source, target, sems.at[i])
        for i, (source, target) in enumerate(((one, one_out), (two, two_out), (three, three_out)))
    ]
    for copy in copies:
        copy.start()
    for copy in copies:
        copy.wait()


def per_device(
    blk_total,
    band_total,
    disp_fwd,
    prev_fwd,
    disp_adj,
    prev_adj,
    modulus,
    radius,
    step_scale,
    kernel_in,
    buckets,
    halo_count,
    blk_nodes,
    band_nodes,
):
    nodes, coeff_len = disp_fwd.shape[2:]
    half = coeff_len // 2
    width = min(512, half)
    chunks = half // width
    pad = -(-nodes // 16) * 16
    blk_slots = blk_nodes.shape[-1]
    band_slots = band_nodes.shape[-1]
    grad_op, div_op, quad = node_operators(pad)
    table = half_table(half, width)
    anywhere = pl.BlockSpec(memory_space=pl.ANY)
    hbm = pl.BlockSpec(memory_space=pltpu.HBM)
    flat = (nodes * coeff_len // 128, 128)
    out = jax.ShapeDtypeStruct(flat, jnp.float32)
    outs = pl.pallas_call(
        functools.partial(kernel, blk_total, band_total, nodes, pad, width),
        out_shape=(pltpu.VMEM(flat, jnp.float32),) * 3,
        in_specs=[hbm] * 16,
        out_specs=(pl.BlockSpec(memory_space=pltpu.VMEM),) * 3,
        scratch_shapes=[
            pltpu.VMEM((6, *flat), jnp.float32),
            pltpu.VMEM(radius.shape, jnp.float32),
            pltpu.VMEM(step_scale.shape, jnp.float32),
            pltpu.VMEM(buckets.shape, jnp.int32),
            pltpu.VMEM(grad_op.shape, jnp.bfloat16),
            pltpu.VMEM(div_op.shape, jnp.bfloat16),
            pltpu.VMEM(quad.shape, jnp.float32),
            pltpu.SMEM(halo_count.shape, jnp.int32),
            pltpu.SMEM(blk_nodes.shape, jnp.int32),
            pltpu.SMEM(band_nodes.shape, jnp.int32),
            pltpu.VMEM(table.shape, jnp.bfloat16),
            pltpu.VMEM((8 * pad, coeff_len), jnp.bfloat16),
            pltpu.VMEM((8 * pad, half), jnp.bfloat16),
            pltpu.VMEM((chunks, 2, pad, 2 * width), jnp.float32),
            pltpu.VMEM((chunks, 2, 2 * blk_slots, 2 * width), jnp.float32),
            pltpu.VMEM((chunks, 2, 2 * band_slots, 2 * width), jnp.float32),
            pltpu.VMEM((chunks, 2, 2 * blk_slots, 2 * width), jnp.float32),
            pltpu.VMEM((chunks, 2, 2 * band_slots, 2 * width), jnp.float32),
            pltpu.SemaphoreType.DMA((6,)),
            pltpu.SemaphoreType.DMA((9,)),
            pltpu.SemaphoreType.DMA((chunks,)),
            pltpu.SemaphoreType.DMA((chunks, 4)),
            pltpu.SemaphoreType.DMA((chunks, 4)),
        ],
        compiler_params=pltpu.CompilerParams(
            collective_id=0, has_side_effects=True, vmem_limit_bytes=67043328 - 3 * 4 * nodes * coeff_len - 40 * 1024
        ),
    )(
        disp_fwd.reshape(flat),
        prev_fwd.reshape(flat),
        disp_adj.reshape(flat),
        prev_adj.reshape(flat),
        modulus.reshape(flat),
        kernel_in.reshape(flat),
        radius,
        step_scale,
        buckets,
        jnp.asarray(grad_op),
        jnp.asarray(div_op),
        jnp.asarray(quad),
        halo_count,
        blk_nodes,
        band_nodes,
        jnp.asarray(table),
    )
    outs = pl.pallas_call(
        deliver,
        out_shape=(out, out, out),
        in_specs=[pl.BlockSpec(memory_space=pltpu.VMEM)] * 3,
        out_specs=(hbm,) * 3,
        scratch_shapes=[pltpu.SemaphoreType.DMA((3,))],
        compiler_params=pltpu.CompilerParams(vmem_limit_bytes=4 * 1024 * 1024),
    )(*outs)
    return tuple(value.reshape(disp_fwd.shape) for value in outs)


def solution(mesh):
    wide = P("blk", "band", None, None)
    line = P("blk", "band", None)
    in_specs = (wide,) * 5 + (line, line, wide, P("blk", "band"), line, wide, wide)
    return jax.shard_map(
        functools.partial(per_device, mesh.shape["blk"], mesh.shape["band"]),
        mesh=mesh,
        in_specs=in_specs,
        out_specs=(wide,) * 3,
        check_vma=False,
    )
```

profile of v0, /device:TPU:0, one launch (start us, length us, event | category | flops | bytes accessed | tf_op | source)
XLA Modules:
  0.0 17.1 jit_solution(15862382482845022011)
XLA Ops:
  1.3 14.9 %shard_map.175 = (f32[400,128]{1,0:T(8,128)S(1)}, f32[400,128]{1,0:T(8,128)S(1)}, f32[400,128]{1,0:T(8,128)S(1)}) custom-call(f32[400,128]{1,0:T(8,128)} %bitcast.9, f32[400,128]{1,0:T(8,128)} %bitcast.10, f32[400,128]{1,0:T(8,128)} %bitcast.11, f32[400,128]{1,0:T(8,128)} %bitcast.12, f32[400,128]{1,0:T(8,128)} %bitcast.13, f32[400,128]{1,0:T(8,128)} %bitcast.14, ...), custom_call_target="tpu_custom_call" | custom-call | tf_op jit(solution)/shard_map/pallas_call | solution.py:422
  16.2 0.8 %shard_map.176 = (f32[400,128]{1,0:T(8,128)}, f32[400,128]{1,0:T(8,128)}, f32[400,128]{1,0:T(8,128)}) custom-call(f32[400,128]{1,0:T(8,128)S(1)} %get-tuple-element.9.one, f32[400,128]{1,0:T(8,128)S(1)} %get-tuple-element.10.two, f32[400,128]{1,0:T(8,128)S(1)} %get-tuple-element.11.three), custom_call_target="tpu_custom_call" | custom-call | tf_op jit(solution)/shard_map/pallas_call | solution.py:473
where the time goes:
time: 17.2 us; the launch traced here: 17.1 us
  Pallas kernels  15.8 us (92%)
  between operations  1.29 us (8%)
    pallas_call x1, Pallas kernels, per_device(): pl.pallas_call(functools.partial(kernel, blk_total, band_total, nodes, pa...  14.9 us
    pallas_call x1, Pallas kernels, per_device(): pl.pallas_call(deliver, out_shape=(out, out, out), in_specs=[pl.BlockSpec...  0.84 us

commit v1 on v0

v1 whole, which is shorter than its diff:
```python
import functools
import math

import jax
import jax.numpy as jnp
import ml_dtypes
import numpy as np
from jax import lax
from jax.experimental import pallas as pl
from jax.experimental.pallas import tpu as pltpu
from jax.sharding import PartitionSpec as P

MESH = pl.DeviceIdType.MESH
LANES = 128
ORDER = 5


def gll_tables():
    inner_root = math.sqrt(3.0 / 7.0)
    points = np.array([-1.0, -inner_root, 0.0, inner_root, 1.0])
    weights = np.array([0.1, 49.0 / 90.0, 32.0 / 45.0, 49.0 / 90.0, 0.1])
    legendre = (35.0 * points**4 - 30.0 * points**2 + 3.0) / 8.0
    derivative = np.zeros((5, 5))
    for target in range(5):
        for source in range(5):
            if target != source:
                derivative[target, source] = (
                    legendre[target] / legendre[source] / (points[target] - points[source])
                )
    derivative[0, 0] = -5.0
    derivative[4, 4] = 5.0
    return derivative.astype(np.float32), np.outer(weights, weights).astype(np.float32)


def split_bf16(value):
    high = value.astype(np.float32).astype(ml_dtypes.bfloat16)
    low = (value.astype(np.float32) - high.astype(np.float32)).astype(ml_dtypes.bfloat16)
    return high, low


def stage_tables(tiles):
    total = tiles * LANES
    group = LANES // tiles
    eye = np.eye(group)
    angle = 2.0 * math.pi * np.outer(np.arange(tiles), np.arange(tiles // 2)) / tiles
    cos, sin = np.cos(angle), np.sin(angle)
    fold = np.block([[cos, -sin], [sin, cos]])
    first = np.kron(eye, fold)
    last = np.zeros((group, tiles, 2, group, tiles))
    for v in range(group):
        last[v, :, :, v, :] = fold.T.reshape(tiles, 2, tiles)
    last = last.reshape(LANES, 2 * LANES)
    kb = (np.arange(tiles)[None] * group + np.arange(group)[:, None]).reshape(-1)
    angle = 2.0 * math.pi * ((kb[:, None] * np.arange(LANES)[None]) % LANES) / LANES
    wide = np.concatenate([np.cos(angle), -np.sin(angle)], axis=1) * math.sqrt(2.0 / total)
    angle = 2.0 * math.pi * np.outer(np.arange(tiles), np.arange(LANES)) / total
    turn = np.stack([np.cos(angle), np.sin(angle)])
    turn_t = np.tile(turn.transpose(0, 2, 1), (1, 1, group))
    bf16 = ml_dtypes.bfloat16
    return (
        np.concatenate(split_bf16(first), axis=1),
        wide.astype(np.float32).astype(bf16),
        wide.T.astype(np.float32).astype(bf16),
        np.concatenate(split_bf16(last), axis=1),
        np.concatenate([turn.reshape(2 * tiles, LANES), turn_t.reshape(2 * LANES, LANES)]).astype(np.float32),
    )


def mm(lhs, rhs):
    return jnp.dot(lhs, rhs, preferred_element_type=jnp.float32)


def mm_nt(lhs, rhs):
    return lax.dot_general(lhs, rhs, (((1,), (1,)), ((), ())), preferred_element_type=jnp.float32)


def swap_granules(parts, tiles):
    parts = list(parts)
    lane = lax.broadcasted_iota(jnp.int32, parts[0].shape, 1)
    bit = len(parts) // 2
    while bit:
        upper = ((lane // tiles) & bit) != 0
        for a in range(len(parts)):
            if not a & bit:
                one, two = parts[a], parts[a | bit]
                parts[a] = jnp.where(upper, pltpu.roll(two, bit * tiles, 1), one)
                parts[a | bit] = jnp.where(upper, two, pltpu.roll(one, LANES - bit * tiles, 1))
        bit //= 2
    return parts


def along_line(table, line):
    sum0, dif0 = line[0] + line[4], line[0] - line[4]
    sum1, dif1 = line[1] + line[3], line[1] - line[3]
    out = [None] * 5
    for i in range(2):
        even = (
            float(table[i, 0] + table[i, 4]) / 2 * sum0
            + float(table[i, 1] + table[i, 3]) / 2 * sum1
            + float(table[i, 2]) * line[2]
        )
        odd = float(table[i, 0] - table[i, 4]) / 2 * dif0 + float(table[i, 1] - table[i, 3]) / 2 * dif1
        out[i], out[4 - i] = odd + even, odd - even
    out[2] = float(table[2, 0]) * dif0 + float(table[2, 1]) * dif1
    return out


def kernel(
    blk_total,
    band_total,
    nodes,
    tiles,
    disp_fwd_hbm,
    modulus_hbm,
    disp_adj_hbm,
    prev_fwd_hbm,
    prev_adj_hbm,
    kernel_in_hbm,
    radius_hbm,
    bucket_hbm,
    step_hbm,
    counts_hbm,
    blk_nodes_hbm,
    band_nodes_hbm,
    first_hbm,
    wide_hbm,
    wide_t_hbm,
    last_hbm,
    turn_hbm,
    next_fwd,
    next_adj,
    kernel_out,
    held,
    radius,
    bucket,
    step_scale,
    counts,
    blk_nodes,
    band_nodes,
    first,
    wide,
    wide_t,
    last,
    turn,
    ratio,
    physical,
    azimuth,
    grad_s,
    grad_z,
    diverge,
    stiff,
    send,
    recv_fwd,
    recv_adj,
    held_sem,
    small_sem,
    send_sem,
    recv_sem,
):
    group = LANES // tiles
    half = tiles // 2
    recv = (recv_fwd, recv_adj)
    side_slots = [blk_nodes.shape[-1]] * 2 + [band_nodes.shape[-1]] * 2
    side_start = [sum(side_slots[:side]) for side in range(4)]
    slots = sum(side_slots)
    derivative, quadrature = gll_tables()
    quad = [float(value) for value in quadrature.reshape(-1)]

    def fetch(i, source, target, sems):
        return pltpu.make_async_copy(source, target, sems.at[i])

    sources = (disp_fwd_hbm, modulus_hbm, disp_adj_hbm, kernel_in_hbm, prev_fwd_hbm, prev_adj_hbm)
    fetches = [fetch(i, source, held.at[i], held_sem) for i, source in enumerate(sources)]
    disp_fwd, modulus, disp_adj, kernel_in, prev_fwd, prev_adj = (held.at[i] for i in range(6))
    small = [
        fetch(i, source, target, small_sem)
        for i, (source, target) in enumerate(
            (
                (radius_hbm, radius),
                (bucket_hbm, bucket),
                (first_hbm, first),
                (turn_hbm, turn),
                (wide_hbm, wide),
                (wide_t_hbm, wide_t),
                (last_hbm, last),
                (step_hbm, step_scale),
                (counts_hbm, counts),
                (blk_nodes_hbm, blk_nodes),
                (band_nodes_hbm, band_nodes),
            )
        )
    ]
    small[0].start()
    small[1].start()
    fetches[0].start()
    for copy in small[2:4]:
        copy.start()
    fetches[1].start()
    for copy in small[4:]:
        copy.start()
    for copy in fetches[2:]:
        copy.start()

    blk = lax.axis_index("blk")
    band = lax.axis_index("band")
    links = [
        (blk > 0, (blk - 1, band)),
        (blk < blk_total - 1, (blk + 1, band)),
        (band > 0, (blk, band - 1)),
        (band < band_total - 1, (blk, band + 1)),
    ]
    barrier = pltpu.get_barrier_semaphore()
    for here, peer in links:

        @pl.when(here)
        def _():
            pl.semaphore_signal(barrier, inc=1, device_id=peer, device_id_type=MESH)

    def rows(side):
        return pl.ds(side_start[side], side_slots[side])

    def transfer(f, side):
        return pltpu.make_async_remote_copy(
            src_ref=send.at[f, rows(side)],
            dst_ref=recv[f].at[rows(side ^ 1)],
            send_sem=send_sem.at[f, side],
            recv_sem=recv_sem.at[f, side ^ 1],
            device_id=links[side][1],
            device_id_type=MESH,
        )

    def arrival(f, side):
        return pltpu.make_async_remote_copy(
            src_ref=send.at[f, rows(side)],
            dst_ref=recv[f].at[rows(side)],
            send_sem=send_sem.at[f, side],
            recv_sem=recv_sem.at[f, side],
            device_id=links[side][1],
            device_id_type=MESH,
        )

    for side in range(4):

        @pl.when(jnp.logical_not(links[side][0]))
        def _():
            for ref in recv:
                ref[rows(side)] = jnp.zeros((side_slots[side], tiles, LANES), jnp.float32)

    for ref in recv:
        ref[slots] = jnp.zeros((tiles, LANES), jnp.float32)

    small[0].wait()
    small[1].wait()
    level = bucket[...]
    orders = half * LANES
    tops = [max(orders // 64, 1), max(orders // 16, 1), max(orders // 4, 1), orders]
    limit = jnp.where(
        level == 0, tops[0], jnp.where(level == 1, tops[1], jnp.where(level == 2, tops[2], tops[3]))
    )
    m = lax.broadcasted_iota(jnp.int32, (half, LANES), 0) * LANES + lax.broadcasted_iota(
        jnp.int32, (half, LANES), 1
    )
    kept = (m < limit).astype(jnp.float32)
    kept_m = m.astype(jnp.float32) * kept
    kept2 = jnp.concatenate([kept, kept], axis=0)
    inv_radius = 1.0 / radius[0]
    for n in range(nodes):
        ratio[n * half : (n + 1) * half, :] = kept_m * inv_radius[:, n : n + 1]

    def node(ref, n):
        return ref[n * tiles : (n + 1) * tiles, :]

    whole_groups = nodes // group
    rest = list(range(whole_groups * group, nodes))
    batches = [
        [[(n, 0) for n in range(g * group, (g + 1) * group)], [(n, 1) for n in range(g * group, (g + 1) * group)]]
        for g in range(whole_groups)
    ]
    spare = [(n, q) for n in rest for q in range(2)]
    for start in range(0, len(spare), group):
        batches.append([spare[start : start + group]])

    def fill(parts, dtype):
        return parts + [jnp.zeros((tiles, LANES), dtype)] * (group - len(parts))

    def coefficients(disp, n, q):
        value = node(disp, n)
        if q == 0:
            return (value * kept2).astype(jnp.bfloat16)
        scale = ratio[n * half : (n + 1) * half, :]
        return jnp.concatenate([value[half:] * -scale, value[:half] * scale], axis=0).astype(jnp.bfloat16)

    def to_samples(f, disp, batch):
        blocks = [
            jnp.concatenate(fill([coefficients(disp, n, q) for n, q in part], jnp.bfloat16), axis=0)
            for part in batch
        ]
        rhs = jnp.concatenate(blocks, axis=1)
        count = max(len(part) for part in batch)
        folded = mm(first[: count * 2 * tiles, :], jnp.concatenate([rhs, rhs], axis=0))
        turned = []
        for b, part in enumerate(batch):
            pieces = []
            for v in range(len(part)):
                at = v * 2 * tiles
                re = folded[at : at + tiles, b * LANES : (b + 1) * LANES]
                im = folded[at + tiles : at + 2 * tiles, b * LANES : (b + 1) * LANES]
                cos, sin = turn[:tiles, :], turn[tiles : 2 * tiles, :]
                pieces.append(
                    jnp.concatenate([re * cos - im * sin, re * sin + im * cos], axis=1).astype(jnp.bfloat16)
                )
            pieces += [jnp.zeros((tiles, 2 * LANES), jnp.bfloat16)] * (group - len(pieces))
            turned.append(jnp.concatenate(pieces, axis=0))
        result = mm_nt(wide[...], jnp.concatenate(turned, axis=0))
        for b, part in enumerate(batch):
            spread = [
                result[g * tiles : (g + 1) * tiles, b * LANES : (b + 1) * LANES] for g in range(group)
            ]
            for (n, q), value in zip(part, swap_granules(spread, tiles)):
                (physical, azimuth.at[f])[q][n * tiles : (n + 1) * tiles, :] = value

    def mix(f):
        for j in range(ORDER):
            line = [ORDER * i + j for i in range(ORDER)]
            grads = along_line(derivative, [node(physical, n) for n in line])
            flux = []
            for n, value in zip(line, grads):
                grad_s[f, n * tiles : (n + 1) * tiles, :] = value
                flux.append(node(modulus, n) * quad[n] * value)
            for n, value in zip(line, along_line(derivative.T, flux)):
                diverge[n * tiles : (n + 1) * tiles, :] = value
        for i in range(ORDER):
            line = [ORDER * i + j for j in range(ORDER)]
            grads = along_line(derivative, [node(physical, n) for n in line])
            flux = []
            for n, value in zip(line, grads):
                grad_z[f, n * tiles : (n + 1) * tiles, :] = value
                flux.append(node(modulus, n) * quad[n] * value)
            for n, value in zip(line, along_line(derivative.T, flux)):
                diverge[n * tiles : (n + 1) * tiles, :] += value

    def stress(f, n, q):
        if q == 0:
            return node(diverge, n)
        return node(modulus, n) * quad[n] * node(azimuth.at[f], n)

    def to_stiff(f, batch):
        blocks = []
        for part in batch:
            parts = fill([stress(f, n, q) for n, q in part], jnp.float32)
            blocks.append(jnp.concatenate(swap_granules(parts, tiles), axis=0).astype(jnp.bfloat16))
        spread = mm(wide_t[...], jnp.concatenate(blocks, axis=1))
        cos, sin = turn[2 * tiles : 2 * tiles + LANES, :], turn[2 * tiles + LANES :, :]
        turned = []
        for b in range(len(batch)):
            re = spread[:LANES, b * LANES : (b + 1) * LANES]
            im = spread[LANES:, b * LANES : (b + 1) * LANES]
            turned.append(jnp.concatenate([re * cos + im * sin, im * cos - re * sin], axis=1).astype(jnp.bfloat16))
        rhs = jnp.concatenate(turned, axis=0)
        count = max(len(part) for part in batch)
        back = mm_nt(last[: count * tiles, :], jnp.concatenate([rhs, rhs], axis=1))
        found = {
            entry: back[v * tiles : (v + 1) * tiles, b * LANES : (b + 1) * LANES]
            for b, part in enumerate(batch)
            for v, entry in enumerate(part)
        }
        for n in sorted({n for n, _ in found}):
            div, phi = found[n, 0], found[n, 1]
            scale = ratio[n * half : (n + 1) * half, :]
            stiff[f, n, :half, :] = kept * div[:half] + scale * phi[half:]
            stiff[f, n, half:, :] = kept * div[half:] - scale * phi[:half]

    fields = ((disp_fwd, prev_fwd, next_fwd), (disp_adj, prev_adj, next_adj))
    for f, (disp, _, _) in enumerate(fields):
        if f == 0:
            fetches[0].wait()
            for copy in small[2:]:
                copy.wait()
        else:
            fetches[2].wait()
        for batch in batches:
            to_samples(f, disp, batch)
        if f == 0:
            fetches[1].wait()
        mix(f)
        for batch in batches:
            to_stiff(f, batch)
        if f == 0:
            pl.semaphore_wait(barrier, sum(here.astype(jnp.int32) for here, _ in links))
        for side in range(4):
            lists = blk_nodes if side < 2 else band_nodes
            for s in range(side_slots[side]):
                send[f, side_start[side] + s] = stiff[f, lists[0, 0, side % 2, s]]

            @pl.when(links[side][0])
            def _():
                transfer(f, side).start()

    owners = [
        jnp.where(s < counts[0, 0, side], (blk_nodes, band_nodes)[side // 2][0, 0, side % 2, s], -1)
        for side in range(4)
        for s in range(side_slots[side])
    ]
    slot_of = []
    for n in range(nodes):
        found = jnp.int32(slots)
        for s, owner in enumerate(owners):
            found = jnp.where(owner == n, s, found)
        slot_of.append(found)

    fetches[3].wait()
    for n in range(nodes):
        product = (
            node(grad_s.at[0], n) * node(grad_s.at[1], n)
            + node(grad_z.at[0], n) * node(grad_z.at[1], n)
            + node(azimuth.at[0], n) * node(azimuth.at[1], n)
        )
        kernel_out[n * tiles : (n + 1) * tiles, :] = node(kernel_in, n) - quad[n] * product

    fetches[4].wait()
    fetches[5].wait()
    for f, (disp, prev, out) in enumerate(fields):
        for n in range(nodes):
            now = node(disp, n)
            value = now + now - node(prev, n) - step_scale[0, 0, n] * stiff[f, n]
            out[n * tiles : (n + 1) * tiles, :] = kept2 * value

    for f, (_, _, out) in enumerate(fields):
        for side in range(4):

            @pl.when(links[side][0])
            def _():
                arrival(f, side).wait_recv()

        for n in range(nodes):
            out[n * tiles : (n + 1) * tiles, :] -= kept2 * step_scale[0, 0, n] * recv[f][slot_of[n]]
    for f in range(2):
        for side in range(4):

            @pl.when(links[side][0])
            def _():
                transfer(f, side).wait_send()


def deliver(one, two, three, one_out, two_out, three_out, sems):
    copies = [
        pltpu.make_async_copy(source, target, sems.at[i])
        for i, (source, target) in enumerate(((one, one_out), (two, two_out), (three, three_out)))
    ]
    for copy in copies:
        copy.start()
    for copy in copies:
        copy.wait()


def per_device(
    blk_total,
    band_total,
    disp_fwd,
    prev_fwd,
    disp_adj,
    prev_adj,
    modulus,
    radius,
    step_scale,
    kernel_in,
    buckets,
    halo_count,
    blk_nodes,
    band_nodes,
):
    nodes, coeff_len = disp_fwd.shape[2:]
    tiles = coeff_len // LANES
    slots = 2 * (blk_nodes.shape[-1] + band_nodes.shape[-1])
    first, wide, wide_t, last, turn = stage_tables(tiles)
    hbm = pl.BlockSpec(memory_space=pltpu.HBM)
    vmem = pl.BlockSpec(memory_space=pltpu.VMEM)
    flat = (nodes * tiles, LANES)
    out = jax.ShapeDtypeStruct(flat, jnp.float32)
    outs = pl.pallas_call(
        functools.partial(kernel, blk_total, band_total, nodes, tiles),
        out_shape=(pltpu.VMEM(flat, jnp.float32),) * 3,
        in_specs=[hbm] * 17,
        out_specs=(vmem,) * 3,
        scratch_shapes=[
            pltpu.VMEM((6, *flat), jnp.float32),
            pltpu.VMEM(radius.shape, jnp.float32),
            pltpu.VMEM(buckets.shape, jnp.int32),
            pltpu.SMEM(step_scale.shape, jnp.float32),
            pltpu.SMEM(halo_count.shape, jnp.int32),
            pltpu.SMEM(blk_nodes.shape, jnp.int32),
            pltpu.SMEM(band_nodes.shape, jnp.int32),
            pltpu.VMEM(first.shape, jnp.bfloat16),
            pltpu.VMEM(wide.shape, jnp.bfloat16),
            pltpu.VMEM(wide_t.shape, jnp.bfloat16),
            pltpu.VMEM(last.shape, jnp.bfloat16),
            pltpu.VMEM(turn.shape, jnp.float32),
            pltpu.VMEM((nodes * tiles // 2, LANES), jnp.float32),
            pltpu.VMEM(flat, jnp.float32),
            pltpu.VMEM((2, *flat), jnp.float32),
            pltpu.VMEM((2, *flat), jnp.float32),
            pltpu.VMEM((2, *flat), jnp.float32),
            pltpu.VMEM(flat, jnp.float32),
            pltpu.VMEM((2, nodes, tiles, LANES), jnp.float32),
            pltpu.VMEM((2, slots, tiles, LANES), jnp.float32),
            pltpu.VMEM((slots + 1, tiles, LANES), jnp.float32),
            pltpu.VMEM((slots + 1, tiles, LANES), jnp.float32),
            pltpu.SemaphoreType.DMA((6,)),
            pltpu.SemaphoreType.DMA((11,)),
            pltpu.SemaphoreType.DMA((2, 4)),
            pltpu.SemaphoreType.DMA((2, 4)),
        ],
        compiler_params=pltpu.CompilerParams(
            collective_id=0,
            has_side_effects=True,
            vmem_limit_bytes=67043328 - 3 * 4 * nodes * coeff_len - 40 * 1024,
        ),
    )(
        disp_fwd.reshape(flat),
        modulus.reshape(flat),
        disp_adj.reshape(flat),
        prev_fwd.reshape(flat),
        prev_adj.reshape(flat),
        kernel_in.reshape(flat),
        radius,
        buckets,
        step_scale,
        halo_count,
        blk_nodes,
        band_nodes,
        jnp.asarray(first),
        jnp.asarray(wide),
        jnp.asarray(wide_t),
        jnp.asarray(last),
        jnp.asarray(turn),
    )
    outs = pl.pallas_call(
        deliver,
        out_shape=(out, out, out),
        in_specs=[vmem] * 3,
        out_specs=(hbm,) * 3,
        scratch_shapes=[pltpu.SemaphoreType.DMA((3,))],
        compiler_params=pltpu.CompilerParams(vmem_limit_bytes=4 * 1024 * 1024),
    )(*outs)
    return tuple(value.reshape(disp_fwd.shape) for value in outs)


def solution(mesh):
    wide = P("blk", "band", None, None)
    line = P("blk", "band", None)
    in_specs = (wide,) * 5 + (line, line, wide, P("blk", "band"), line, wide, wide)
    return jax.shard_map(
        functools.partial(per_device, mesh.shape["blk"], mesh.shape["band"]),
        mesh=mesh,
        in_specs=in_specs,
        out_specs=(wide,) * 3,
        check_vma=False,
    )
```

time: 17.2 us -> 14.4 us (0.84)
  Pallas kernels: 15.8 us -> 12.9 us
    pallas_call x2, Pallas kernels: 15.8 us -> 12.9 us  [the longest x1 12.1 us: per_device(): pl.pallas_call(functools.partial(kernel, blk_total, band_total, nodes, ti...]
where the time goes in v1:
time: 14.4 us; the launch traced here: 14.2 us
  Pallas kernels  12.9 us (90%)
  between operations  1.29 us (9%)
    pallas_call x1, Pallas kernels, per_device(): pl.pallas_call(functools.partial(kernel, blk_total, band_total, nodes, ti...  12.1 us
    pallas_call x1, Pallas kernels, per_device(): pl.pallas_call(deliver, out_shape=(out, out, out), in_specs=[vmem] * 3, o...  0.84 us

profile of v1, /device:TPU:0, one launch (start us, length us, event | category | flops | bytes accessed | tf_op | source)
XLA Modules:
  0.0 14.2 jit_solution(7088464165900278518)
XLA Ops:
  1.3 12.1 %shard_map.184 = (f32[400,128]{1,0:T(8,128)S(1)}, f32[400,128]{1,0:T(8,128)S(1)}, f32[400,128]{1,0:T(8,128)S(1)}) custom-call(f32[400,128]{1,0:T(8,128)} %bitcast.9, f32[400,128]{1,0:T(8,128)} %bitcast.10, f32[400,128]{1,0:T(8,128)} %bitcast.11, f32[400,128]{1,0:T(8,128)} %bitcast.12, f32[400,128]{1,0:T(8,128)} %bitcast.13, f32[400,128]{1,0:T(8,128)} %bitcast.14, ...), custom_call_target="tpu_custom_call" | custom-call | tf_op jit(solution)/shard_map/pallas_call | solution.py:480
  13.4 0.8 %shard_map.185 = (f32[400,128]{1,0:T(8,128)}, f32[400,128]{1,0:T(8,128)}, f32[400,128]{1,0:T(8,128)}) custom-call(f32[400,128]{1,0:T(8,128)S(1)} %get-tuple-element.9.one, f32[400,128]{1,0:T(8,128)S(1)} %get-tuple-element.10.two, f32[400,128]{1,0:T(8,128)S(1)} %get-tuple-element.11.three), custom_call_target="tpu_custom_call" | custom-call | tf_op jit(solution)/shard_map/pallas_call | solution.py:537

commit v2 on v1

--- a/solution.py
+++ b/solution.py
@@ -32,38 +32,34 @@
     return derivative.astype(np.float32), np.outer(weights, weights).astype(np.float32)
 
 
-def split_bf16(value):
-    high = value.astype(np.float32).astype(ml_dtypes.bfloat16)
-    low = (value.astype(np.float32) - high.astype(np.float32)).astype(ml_dtypes.bfloat16)
-    return high, low
+def rounded(value):
+    return np.asarray(value, np.float32).astype(ml_dtypes.bfloat16)
+
+
+def best_scale(value):
+    levels = np.unique(np.round(np.abs(value), 12))
+    factors = 1.0 + np.arange(10000) / 10000.0
+    scaled = factors[:, None] * levels[None]
+    loss = ((rounded(scaled).astype(np.float64) - scaled) ** 2).sum(axis=1) / factors**2
+    return float(factors[np.argmin(loss)])
 
 
 def stage_tables(tiles):
     total = tiles * LANES
     group = LANES // tiles
-    eye = np.eye(group)
     angle = 2.0 * math.pi * np.outer(np.arange(tiles), np.arange(tiles // 2)) / tiles
     cos, sin = np.cos(angle), np.sin(angle)
     fold = np.block([[cos, -sin], [sin, cos]])
-    first = np.kron(eye, fold)
-    last = np.zeros((group, tiles, 2, group, tiles))
-    for v in range(group):
-        last[v, :, :, v, :] = fold.T.reshape(tiles, 2, tiles)
-    last = last.reshape(LANES, 2 * LANES)
     kb = (np.arange(tiles)[None] * group + np.arange(group)[:, None]).reshape(-1)
     angle = 2.0 * math.pi * ((kb[:, None] * np.arange(LANES)[None]) % LANES) / LANES
     wide = np.concatenate([np.cos(angle), -np.sin(angle)], axis=1) * math.sqrt(2.0 / total)
     angle = 2.0 * math.pi * np.outer(np.arange(tiles), np.arange(LANES)) / total
-    turn = np.stack([np.cos(angle), np.sin(angle)])
-    turn_t = np.tile(turn.transpose(0, 2, 1), (1, 1, group))
-    bf16 = ml_dtypes.bfloat16
-    return (
-        np.concatenate(split_bf16(first), axis=1),
-        wide.astype(np.float32).astype(bf16),
-        wide.T.astype(np.float32).astype(bf16),
-        np.concatenate(split_bf16(last), axis=1),
-        np.concatenate([turn.reshape(2 * tiles, LANES), turn_t.reshape(2 * LANES, LANES)]).astype(np.float32),
-    )
+    turn = np.concatenate([np.cos(angle), np.sin(angle)])
+    fold_scale, wide_scale = best_scale(fold), best_scale(wide)
+    first = rounded(np.tile(fold * fold_scale, (1, group)))
+    last = rounded(np.tile(fold.T * fold_scale, (1, group)))
+    turn = (turn / (fold_scale * wide_scale)).astype(np.float32)
+    return first, last, rounded(wide.T * wide_scale), turn
 
 
 def mm(lhs, rhs):
@@ -72,6 +68,14 @@
 
 def mm_nt(lhs, rhs):
     return lax.dot_general(lhs, rhs, (((1,), (1,)), ((), ())), preferred_element_type=jnp.float32)
+
+
+def blocks_of(tile, group):
+    rows, columns = tile.shape
+    lane = lax.broadcasted_iota(jnp.int32, tile.shape, 1) // (columns // group)
+    value = tile.astype(jnp.float32)
+    parts = [jnp.where(lane == v, value, 0.0).astype(jnp.bfloat16) for v in range(group)]
+    return jnp.concatenate(parts, axis=0)
 
 
 def swap_granules(parts, tiles):
@@ -123,9 +127,8 @@
     blk_nodes_hbm,
     band_nodes_hbm,
     first_hbm,
+    last_hbm,
     wide_hbm,
-    wide_t_hbm,
-    last_hbm,
     turn_hbm,
     next_fwd,
     next_adj,
@@ -138,11 +141,13 @@
     blk_nodes,
     band_nodes,
     first,
+    last,
     wide,
-    wide_t,
-    last,
     turn,
+    first_blocks,
+    last_blocks,
     ratio,
+    weight,
     physical,
     azimuth,
     grad_s,
@@ -179,10 +184,9 @@
                 (radius_hbm, radius),
                 (bucket_hbm, bucket),
                 (first_hbm, first),
+                (last_hbm, last),
                 (turn_hbm, turn),
                 (wide_hbm, wide),
-                (wide_t_hbm, wide_t),
-                (last_hbm, last),
                 (step_hbm, step_scale),
                 (counts_hbm, counts),
                 (blk_nodes_hbm, blk_nodes),
@@ -193,12 +197,10 @@
     small[0].start()
     small[1].start()
     fetches[0].start()
-    for copy in small[2:4]:
+    for copy in small[2:6]:
         copy.start()
     fetches[1].start()
-    for copy in small[4:]:
-        copy.start()
-    for copy in fetches[2:]:
+    for copy in small[6:]:
         copy.start()
 
     blk = lax.axis_index("blk")
@@ -209,6 +211,8 @@
         (band > 0, (blk, band - 1)),
         (band < band_total - 1, (blk, band + 1)),
     ]
+    early = [links[0][0], links[1][0] & (blk != 1), links[2][0], links[3][0]]
+    late = [blk < 0, links[1][0] & (blk == 1)]
     barrier = pltpu.get_barrier_semaphore()
     for here, peer in links:
 
@@ -270,18 +274,22 @@
     def node(ref, n):
         return ref[n * tiles : (n + 1) * tiles, :]
 
-    whole_groups = nodes // group
-    rest = list(range(whole_groups * group, nodes))
-    batches = [
-        [[(n, 0) for n in range(g * group, (g + 1) * group)], [(n, 1) for n in range(g * group, (g + 1) * group)]]
-        for g in range(whole_groups)
-    ]
-    spare = [(n, q) for n in rest for q in range(2)]
-    for start in range(0, len(spare), group):
-        batches.append([spare[start : start + group]])
-
-    def fill(parts, dtype):
-        return parts + [jnp.zeros((tiles, LANES), dtype)] * (group - len(parts))
+    def put(ref, n, value):
+        ref[n * tiles : (n + 1) * tiles, :] = value
+
+    whole = nodes // group * group
+    blocks = [[[(n, q) for n in range(g, g + group)] for g in range(0, whole, group)] for q in range(2)]
+    spare = [(n, q) for n in range(whole, nodes) for q in range(2)]
+    blocks[0] += [spare[g : g + group] for g in range(0, len(spare), group)]
+    batches = [[[part] for part in side] for side in blocks]
+    back_batches = [[[part] for part in side] for side in blocks]
+
+    def stacked(parts):
+        parts = parts + [jnp.zeros(parts[0].shape, parts[0].dtype)] * (group - len(parts))
+        return jnp.concatenate(parts, axis=0)
+
+    def spot(result, b, at, size):
+        return result[at : at + size, b * LANES : (b + 1) * LANES]
 
     def coefficients(disp, n, q):
         value = node(disp, n)
@@ -291,33 +299,31 @@
         return jnp.concatenate([value[half:] * -scale, value[:half] * scale], axis=0).astype(jnp.bfloat16)
 
     def to_samples(f, disp, batch):
-        blocks = [
-            jnp.concatenate(fill([coefficients(disp, n, q) for n, q in part], jnp.bfloat16), axis=0)
-            for part in batch
-        ]
-        rhs = jnp.concatenate(blocks, axis=1)
-        count = max(len(part) for part in batch)
-        folded = mm(first[: count * 2 * tiles, :], jnp.concatenate([rhs, rhs], axis=0))
+        rhs = jnp.concatenate(
+            [stacked([coefficients(disp, n, q) for n, q in part]) for part in batch], axis=1
+        )
+        cos, sin = turn[:tiles, :], turn[tiles:, :]
+        folded = mm(first_blocks[: max(len(part) for part in batch) * 2 * tiles, :], rhs)
         turned = []
         for b, part in enumerate(batch):
-            pieces = []
             for v in range(len(part)):
-                at = v * 2 * tiles
-                re = folded[at : at + tiles, b * LANES : (b + 1) * LANES]
-                im = folded[at + tiles : at + 2 * tiles, b * LANES : (b + 1) * LANES]
-                cos, sin = turn[:tiles, :], turn[tiles : 2 * tiles, :]
-                pieces.append(
+                re = spot(folded, b, v * 2 * tiles, tiles)
+                im = spot(folded, b, (v * 2 + 1) * tiles, tiles)
+                turned.append(
                     jnp.concatenate([re * cos - im * sin, re * sin + im * cos], axis=1).astype(jnp.bfloat16)
                 )
-            pieces += [jnp.zeros((tiles, 2 * LANES), jnp.bfloat16)] * (group - len(pieces))
-            turned.append(jnp.concatenate(pieces, axis=0))
-        result = mm_nt(wide[...], jnp.concatenate(turned, axis=0))
-        for b, part in enumerate(batch):
-            spread = [
-                result[g * tiles : (g + 1) * tiles, b * LANES : (b + 1) * LANES] for g in range(group)
-            ]
-            for (n, q), value in zip(part, swap_granules(spread, tiles)):
-                (physical, azimuth.at[f])[q][n * tiles : (n + 1) * tiles, :] = value
+        result = mm(jnp.concatenate(turned, axis=0), wide[...])
+        for at, (n, q) in enumerate(entry for part in batch for entry in part):
+            put((physical, azimuth.at[f])[q], n, spot(result, 0, at * tiles, tiles))
+
+    def weights():
+        for g in range(0, nodes, group):
+            part = list(range(g, min(g + group, nodes)))
+            parts = [node(modulus, n) for n in part]
+            parts += [jnp.zeros((tiles, LANES), jnp.float32)] * (group - len(part))
+            turned = jnp.concatenate(swap_granules(parts, tiles), axis=0).T
+            for v, n in enumerate(part):
+                put(weight, n, quad[n] * turned[v * tiles : (v + 1) * tiles, :])
 
     def mix(f):
         for j in range(ORDER):
@@ -325,66 +331,71 @@
             grads = along_line(derivative, [node(physical, n) for n in line])
             flux = []
             for n, value in zip(line, grads):
-                grad_s[f, n * tiles : (n + 1) * tiles, :] = value
-                flux.append(node(modulus, n) * quad[n] * value)
+                put(grad_s.at[f], n, value)
+                flux.append(node(weight, n) * value)
             for n, value in zip(line, along_line(derivative.T, flux)):
-                diverge[n * tiles : (n + 1) * tiles, :] = value
+                put(diverge, n, value)
         for i in range(ORDER):
             line = [ORDER * i + j for j in range(ORDER)]
             grads = along_line(derivative, [node(physical, n) for n in line])
             flux = []
             for n, value in zip(line, grads):
-                grad_z[f, n * tiles : (n + 1) * tiles, :] = value
-                flux.append(node(modulus, n) * quad[n] * value)
+                put(grad_z.at[f], n, value)
+                flux.append(node(weight, n) * value)
             for n, value in zip(line, along_line(derivative.T, flux)):
-                diverge[n * tiles : (n + 1) * tiles, :] += value
+                put(diverge, n, node(diverge, n) + value)
 
     def stress(f, n, q):
-        if q == 0:
-            return node(diverge, n)
-        return node(modulus, n) * quad[n] * node(azimuth.at[f], n)
-
-    def to_stiff(f, batch):
-        blocks = []
-        for part in batch:
-            parts = fill([stress(f, n, q) for n, q in part], jnp.float32)
-            blocks.append(jnp.concatenate(swap_granules(parts, tiles), axis=0).astype(jnp.bfloat16))
-        spread = mm(wide_t[...], jnp.concatenate(blocks, axis=1))
-        cos, sin = turn[2 * tiles : 2 * tiles + LANES, :], turn[2 * tiles + LANES :, :]
-        turned = []
-        for b in range(len(batch)):
-            re = spread[:LANES, b * LANES : (b + 1) * LANES]
-            im = spread[LANES:, b * LANES : (b + 1) * LANES]
-            turned.append(jnp.concatenate([re * cos + im * sin, im * cos - re * sin], axis=1).astype(jnp.bfloat16))
-        rhs = jnp.concatenate(turned, axis=0)
-        count = max(len(part) for part in batch)
-        back = mm_nt(last[: count * tiles, :], jnp.concatenate([rhs, rhs], axis=1))
-        found = {
-            entry: back[v * tiles : (v + 1) * tiles, b * LANES : (b + 1) * LANES]
-            for b, part in enumerate(batch)
-            for v, entry in enumerate(part)
-        }
-        for n in sorted({n for n, _ in found}):
+        value = node(weight, n) * node(azimuth.at[f], n) if q else node(diverge, n)
+        return value.astype(jnp.bfloat16)
+
+    def to_coefficients(f, batch, found):
+        entries = [entry for part in batch for entry in part]
+        cos, sin = turn[:tiles, :], turn[tiles:, :]
+        spread = mm_nt(jnp.concatenate([stress(f, n, q) for n, q in entries], axis=0), wide[...])
+        turned = {}
+        for at, entry in enumerate(entries):
+            re = spot(spread, 0, at * tiles, tiles)
+            im = spot(spread, 1, at * tiles, tiles)
+            turned[entry] = jnp.concatenate([re * cos + im * sin, im * cos - re * sin], axis=0).astype(
+                jnp.bfloat16
+            )
+        rhs = jnp.concatenate([stacked([turned[entry] for entry in part]) for part in batch], axis=1)
+        back = mm(last_blocks[: max(len(part) for part in batch) * tiles, :], rhs)
+        for b, part in enumerate(batch):
+            for v, entry in enumerate(part):
+                found[entry] = spot(back, b, v * tiles, tiles)
+
+    fields = ((disp_fwd, prev_fwd, next_fwd), (disp_adj, prev_adj, next_adj))
+    for f, (disp, _, _) in enumerate(fields):
+        if f == 0:
+            for copy in small[2:]:
+                copy.wait()
+            first_blocks[...] = blocks_of(first[...], group)
+            last_blocks[...] = blocks_of(last[...], group)
+            fetches[0].wait()
+            fetches[1].wait()
+            for copy in fetches[2:]:
+                copy.start()
+        else:
+            fetches[2].wait()
+        for batch in batches[0]:
+            to_samples(f, disp, batch)
+        for batch in batches[1]:
+            to_samples(f, disp, batch)
+        if f == 0:
+            weights()
+        found = {}
+        for batch in back_batches[1]:
+            to_coefficients(f, batch, found)
+        mix(f)
+        for batch in back_batches[0]:
+            to_coefficients(f, batch, found)
+        for n in range(nodes):
             div, phi = found[n, 0], found[n, 1]
             scale = ratio[n * half : (n + 1) * half, :]
             stiff[f, n, :half, :] = kept * div[:half] + scale * phi[half:]
             stiff[f, n, half:, :] = kept * div[half:] - scale * phi[:half]
-
-    fields = ((disp_fwd, prev_fwd, next_fwd), (disp_adj, prev_adj, next_adj))
-    for f, (disp, _, _) in enumerate(fields):
-        if f == 0:
-            fetches[0].wait()
-            for copy in small[2:]:
-                copy.wait()
-        else:
-            fetches[2].wait()
-        for batch in batches:
-            to_samples(f, disp, batch)
-        if f == 0:
-            fetches[1].wait()
-        mix(f)
-        for batch in batches:
-            to_stiff(f, batch)
         if f == 0:
             pl.semaphore_wait(barrier, sum(here.astype(jnp.int32) for here, _ in links))
         for side in range(4):
@@ -392,9 +403,43 @@
             for s in range(side_slots[side]):
                 send[f, side_start[side] + s] = stiff[f, lists[0, 0, side % 2, s]]
 
-            @pl.when(links[side][0])
+            @pl.when(early[side])
             def _():
                 transfer(f, side).start()
+
+    def follow(f):
+        for side in range(2):
+
+            @pl.when(late[side])
+            def _():
+                transfer(f, side).start()
+
+    follow(0)
+    follow(1)
+    fetches[3].wait()
+    for g in range(0, nodes, group):
+        part = list(range(g, min(g + group, nodes)))
+        products = [
+            quad[n]
+            * (
+                node(grad_s.at[0], n) * node(grad_s.at[1], n)
+                + node(grad_z.at[0], n) * node(grad_z.at[1], n)
+                + node(azimuth.at[0], n) * node(azimuth.at[1], n)
+            )
+            for n in part
+        ]
+        turned = stacked(products).T
+        spread = swap_granules([turned[h * tiles : (h + 1) * tiles, :] for h in range(group)], tiles)
+        for n, value in zip(part, spread):
+            put(kernel_out, n, node(kernel_in, n) - value)
+
+    fetches[4].wait()
+    fetches[5].wait()
+    for f, (disp, prev, out) in enumerate(fields):
+        for n in range(nodes):
+            now = node(disp, n)
+            value = now + now - node(prev, n) - step_scale[0, 0, n] * stiff[f, n]
+            out[n * tiles : (n + 1) * tiles, :] = kept2 * value
 
     owners = [
         jnp.where(s < counts[0, 0, side], (blk_nodes, band_nodes)[side // 2][0, 0, side % 2, s], -1)
@@ -407,23 +452,6 @@
         for s, owner in enumerate(owners):
             found = jnp.where(owner == n, s, found)
         slot_of.append(found)
-
-    fetches[3].wait()
-    for n in range(nodes):
-        product = (
-            node(grad_s.at[0], n) * node(grad_s.at[1], n)
-            + node(grad_z.at[0], n) * node(grad_z.at[1], n)
-            + node(azimuth.at[0], n) * node(azimuth.at[1], n)
-        )
-        kernel_out[n * tiles : (n + 1) * tiles, :] = node(kernel_in, n) - quad[n] * product
-
-    fetches[4].wait()
-    fetches[5].wait()
-    for f, (disp, prev, out) in enumerate(fields):
-        for n in range(nodes):
-            now = node(disp, n)
-            value = now + now - node(prev, n) - step_scale[0, 0, n] * stiff[f, n]
-            out[n * tiles : (n + 1) * tiles, :] = kept2 * value
 
     for f, (_, _, out) in enumerate(fields):
         for side in range(4):
@@ -472,7 +500,7 @@
     nodes, coeff_len = disp_fwd.shape[2:]
     tiles = coeff_len // LANES
     slots = 2 * (blk_nodes.shape[-1] + band_nodes.shape[-1])
-    first, wide, wide_t, last, turn = stage_tables(tiles)
+    first, last, wide, turn = stage_tables(tiles)
     hbm = pl.BlockSpec(memory_space=pltpu.HBM)
     vmem = pl.BlockSpec(memory_space=pltpu.VMEM)
     flat = (nodes * tiles, LANES)
@@ -480,7 +508,7 @@
     outs = pl.pallas_call(
         functools.partial(kernel, blk_total, band_total, nodes, tiles),
         out_shape=(pltpu.VMEM(flat, jnp.float32),) * 3,
-        in_specs=[hbm] * 17,
+        in_specs=[hbm] * 16,
         out_specs=(vmem,) * 3,
         scratch_shapes=[
             pltpu.VMEM((6, *flat), jnp.float32),
@@ -491,11 +519,13 @@
             pltpu.SMEM(blk_nodes.shape, jnp.int32),
             pltpu.SMEM(band_nodes.shape, jnp.int32),
             pltpu.VMEM(first.shape, jnp.bfloat16),
+            pltpu.VMEM(last.shape, jnp.bfloat16),
             pltpu.VMEM(wide.shape, jnp.bfloat16),
-            pltpu.VMEM(wide_t.shape, jnp.bfloat16),
-            pltpu.VMEM(last.shape, jnp.bfloat16),
             pltpu.VMEM(turn.shape, jnp.float32),
+            pltpu.VMEM((2 * LANES, LANES), jnp.bfloat16),
+            pltpu.VMEM((LANES, 2 * LANES), jnp.bfloat16),
             pltpu.VMEM((nodes * tiles // 2, LANES), jnp.float32),
+            pltpu.VMEM(flat, jnp.float32),
             pltpu.VMEM(flat, jnp.float32),
             pltpu.VMEM((2, *flat), jnp.float32),
             pltpu.VMEM((2, *flat), jnp.float32),
@@ -506,7 +536,7 @@
             pltpu.VMEM((slots + 1, tiles, LANES), jnp.float32),
             pltpu.VMEM((slots + 1, tiles, LANES), jnp.float32),
             pltpu.SemaphoreType.DMA((6,)),
-            pltpu.SemaphoreType.DMA((11,)),
+            pltpu.SemaphoreType.DMA((10,)),
             pltpu.SemaphoreType.DMA((2, 4)),
             pltpu.SemaphoreType.DMA((2, 4)),
         ],
@@ -529,9 +559,8 @@
         blk_nodes,
         band_nodes,
         jnp.asarray(first),
+        jnp.asarray(last),
         jnp.asarray(wide),
-        jnp.asarray(wide_t),
-        jnp.asarray(last),
         jnp.asarray(turn),
     )
     outs = pl.pallas_call(

time: 14.4 us -> 12.7 us (0.88)
  the two profiles are of different devices: /device:TPU:0 before, /device:TPU:4 now
where the time goes in v2:
time: 12.7 us; the launch traced here: 12.5 us
  Pallas kernels  11.2 us (88%)
  between operations  1.29 us (10%)
    pallas_call x1, Pallas kernels, per_device(): pl.pallas_call(functools.partial(kernel, blk_total, band_total, nodes, ti...  10.4 us
    pallas_call x1, Pallas kernels, per_device(): pl.pallas_call(deliver, out_shape=(out, out, out), in_specs=[vmem] * 3, o...  0.84 us

profile of v2, /device:TPU:4, one launch (start us, length us, event | category | flops | bytes accessed | tf_op | source)
XLA Modules:
  0.0 12.5 jit_solution(16326004613357340288)
XLA Ops:
  1.3 10.4 %shard_map.175 = (f32[400,128]{1,0:T(8,128)S(1)}, f32[400,128]{1,0:T(8,128)S(1)}, f32[400,128]{1,0:T(8,128)S(1)}) custom-call(f32[400,128]{1,0:T(8,128)} %bitcast.9, f32[400,128]{1,0:T(8,128)} %bitcast.10, f32[400,128]{1,0:T(8,128)} %bitcast.11, f32[400,128]{1,0:T(8,128)} %bitcast.12, f32[400,128]{1,0:T(8,128)} %bitcast.13, f32[400,128]{1,0:T(8,128)} %bitcast.14, ...), custom_call_target="tpu_custom_call" | custom-call | tf_op jit(solution)/shard_map/pallas_call | solution.py:508
  11.7 0.8 %shard_map.176 = (f32[400,128]{1,0:T(8,128)}, f32[400,128]{1,0:T(8,128)}, f32[400,128]{1,0:T(8,128)}) custom-call(f32[400,128]{1,0:T(8,128)S(1)} %get-tuple-element.9.one, f32[400,128]{1,0:T(8,128)S(1)} %get-tuple-element.10.two, f32[400,128]{1,0:T(8,128)S(1)} %get-tuple-element.11.three), custom_call_target="tpu_custom_call" | custom-call | tf_op jit(solution)/shard_map/pallas_call | solution.py:566

commit v3 on v2

--- a/solution.py
+++ b/solution.py
@@ -298,23 +298,26 @@
         scale = ratio[n * half : (n + 1) * half, :]
         return jnp.concatenate([value[half:] * -scale, value[:half] * scale], axis=0).astype(jnp.bfloat16)
 
-    def to_samples(f, disp, batch):
-        rhs = jnp.concatenate(
-            [stacked([coefficients(disp, n, q) for n, q in part]) for part in batch], axis=1
-        )
+    def to_samples(f, disp, group_batches):
+        folds = []
+        for batch in group_batches:
+            rhs = jnp.concatenate(
+                [stacked([coefficients(disp, n, q) for n, q in part]) for part in batch], axis=1
+            )
+            folds.append(mm(first_blocks[: max(len(part) for part in batch) * 2 * tiles, :], rhs))
         cos, sin = turn[:tiles, :], turn[tiles:, :]
-        folded = mm(first_blocks[: max(len(part) for part in batch) * 2 * tiles, :], rhs)
-        turned = []
-        for b, part in enumerate(batch):
-            for v in range(len(part)):
-                re = spot(folded, b, v * 2 * tiles, tiles)
-                im = spot(folded, b, (v * 2 + 1) * tiles, tiles)
-                turned.append(
-                    jnp.concatenate([re * cos - im * sin, re * sin + im * cos], axis=1).astype(jnp.bfloat16)
-                )
-        result = mm(jnp.concatenate(turned, axis=0), wide[...])
-        for at, (n, q) in enumerate(entry for part in batch for entry in part):
-            put((physical, azimuth.at[f])[q], n, spot(result, 0, at * tiles, tiles))
+        for batch, folded in zip(group_batches, folds):
+            turned = []
+            for b, part in enumerate(batch):
+                for v in range(len(part)):
+                    re = spot(folded, b, v * 2 * tiles, tiles)
+                    im = spot(folded, b, (v * 2 + 1) * tiles, tiles)
+                    turned.append(
+                        jnp.concatenate([re * cos - im * sin, re * sin + im * cos], axis=1).astype(jnp.bfloat16)
+                    )
+            result = mm(jnp.concatenate(turned, axis=0), wide[...])
+            for at, (n, q) in enumerate(entry for part in batch for entry in part):
+                put((physical, azimuth.at[f])[q], n, spot(result, 0, at * tiles, tiles))
 
     def weights():
         for g in range(0, nodes, group):
@@ -349,54 +352,54 @@
         value = node(weight, n) * node(azimuth.at[f], n) if q else node(diverge, n)
         return value.astype(jnp.bfloat16)
 
-    def to_coefficients(f, batch, found):
-        entries = [entry for part in batch for entry in part]
+    def to_coefficients(f, group_batches, found):
+        spreads = []
+        for batch in group_batches:
+            entries = [entry for part in batch for entry in part]
+            spreads.append(mm_nt(jnp.concatenate([stress(f, n, q) for n, q in entries], axis=0), wide[...]))
         cos, sin = turn[:tiles, :], turn[tiles:, :]
-        spread = mm_nt(jnp.concatenate([stress(f, n, q) for n, q in entries], axis=0), wide[...])
-        turned = {}
-        for at, entry in enumerate(entries):
-            re = spot(spread, 0, at * tiles, tiles)
-            im = spot(spread, 1, at * tiles, tiles)
-            turned[entry] = jnp.concatenate([re * cos + im * sin, im * cos - re * sin], axis=0).astype(
-                jnp.bfloat16
-            )
-        rhs = jnp.concatenate([stacked([turned[entry] for entry in part]) for part in batch], axis=1)
-        back = mm(last_blocks[: max(len(part) for part in batch) * tiles, :], rhs)
-        for b, part in enumerate(batch):
-            for v, entry in enumerate(part):
-                found[entry] = spot(back, b, v * tiles, tiles)
+        for batch, spread in zip(group_batches, spreads):
+            turned = {}
+            for at, entry in enumerate(entry for part in batch for entry in part):
+                re = spot(spread, 0, at * tiles, tiles)
+                im = spot(spread, 1, at * tiles, tiles)
+                turned[entry] = jnp.concatenate([re * cos + im * sin, im * cos - re * sin], axis=0).astype(
+                    jnp.bfloat16
+                )
+            rhs = jnp.concatenate([stacked([turned[entry] for entry in part]) for part in batch], axis=1)
+            back = mm(last_blocks[: max(len(part) for part in batch) * tiles, :], rhs)
+            for b, part in enumerate(batch):
+                for v, entry in enumerate(part):
+                    found[entry] = spot(back, b, v * tiles, tiles)
 
     fields = ((disp_fwd, prev_fwd, next_fwd), (disp_adj, prev_adj, next_adj))
     for f, (disp, _, _) in enumerate(fields):
         if f == 0:
-            for copy in small[2:]:
+            for copy in small[2:6]:
                 copy.wait()
-            first_blocks[...] = blocks_of(first[...], group)
-            last_blocks[...] = blocks_of(last[...], group)
             fetches[0].wait()
             fetches[1].wait()
             for copy in fetches[2:]:
                 copy.start()
+            first_blocks[...] = blocks_of(first[...], group)
+            last_blocks[...] = blocks_of(last[...], group)
         else:
             fetches[2].wait()
-        for batch in batches[0]:
-            to_samples(f, disp, batch)
-        for batch in batches[1]:
-            to_samples(f, disp, batch)
+        to_samples(f, disp, batches[0])
+        to_samples(f, disp, batches[1])
         if f == 0:
             weights()
         found = {}
-        for batch in back_batches[1]:
-            to_coefficients(f, batch, found)
         mix(f)
-        for batch in back_batches[0]:
-            to_coefficients(f, batch, found)
+        to_coefficients(f, back_batches[1] + back_batches[0], found)
         for n in range(nodes):
             div, phi = found[n, 0], found[n, 1]
             scale = ratio[n * half : (n + 1) * half, :]
             stiff[f, n, :half, :] = kept * div[:half] + scale * phi[half:]
             stiff[f, n, half:, :] = kept * div[half:] - scale * phi[:half]
         if f == 0:
+            for copy in small[6:]:
+                copy.wait()
             pl.semaphore_wait(barrier, sum(here.astype(jnp.int32) for here, _ in links))
         for side in range(4):
             lists = blk_nodes if side < 2 else band_nodes

time: 12.7 us -> 12.7 us (level)
  no operation moved by 1% of the time
where the time goes in v3:
time: 12.7 us; the launch traced here: 12.5 us
  Pallas kernels  11.2 us (88%)
  between operations  1.29 us (10%)
    pallas_call x1, Pallas kernels, per_device(): pl.pallas_call(functools.partial(kernel, blk_total, band_total, nodes, ti...  10.4 us
    pallas_call x1, Pallas kernels, per_device(): pl.pallas_call(deliver, out_shape=(out, out, out), in_specs=[vmem] * 3, o...  0.84 us

profile of v3, /device:TPU:4, one launch (start us, length us, event | category | flops | bytes accessed | tf_op | source)
XLA Modules:
  0.0 12.5 jit_solution(14224905262705818079)
XLA Ops:
  1.3 10.4 %shard_map.175 = (f32[400,128]{1,0:T(8,128)S(1)}, f32[400,128]{1,0:T(8,128)S(1)}, f32[400,128]{1,0:T(8,128)S(1)}) custom-call(f32[400,128]{1,0:T(8,128)} %bitcast.9, f32[400,128]{1,0:T(8,128)} %bitcast.10, f32[400,128]{1,0:T(8,128)} %bitcast.11, f32[400,128]{1,0:T(8,128)} %bitcast.12, f32[400,128]{1,0:T(8,128)} %bitcast.13, f32[400,128]{1,0:T(8,128)} %bitcast.14, ...), custom_call_target="tpu_custom_call" | custom-call | tf_op jit(solution)/shard_map/pallas_call | solution.py:511
  11.7 0.8 %shard_map.176 = (f32[400,128]{1,0:T(8,128)}, f32[400,128]{1,0:T(8,128)}, f32[400,128]{1,0:T(8,128)}) custom-call(f32[400,128]{1,0:T(8,128)S(1)} %get-tuple-element.9.one, f32[400,128]{1,0:T(8,128)S(1)} %get-tuple-element.10.two, f32[400,128]{1,0:T(8,128)S(1)} %get-tuple-element.11.three), custom_call_target="tpu_custom_call" | custom-call | tf_op jit(solution)/shard_map/pallas_call | solution.py:569

commit v4 on v3

--- a/solution.py
+++ b/solution.py
@@ -385,8 +385,7 @@
             last_blocks[...] = blocks_of(last[...], group)
         else:
             fetches[2].wait()
-        to_samples(f, disp, batches[0])
-        to_samples(f, disp, batches[1])
+        to_samples(f, disp, batches[0] + batches[1])
         if f == 0:
             weights()
         found = {}

time: 12.7 us -> 12.6 us (level)
  no operation moved by 1% of the time
where the time goes in v4:
time: 12.6 us; the launch traced here: 12.4 us
  Pallas kernels  11.1 us (88%)
  between operations  1.29 us (10%)
    pallas_call x1, Pallas kernels, per_device(): pl.pallas_call(functools.partial(kernel, blk_total, band_total, nodes, ti...  10.3 us
    pallas_call x1, Pallas kernels, per_device(): pl.pallas_call(deliver, out_shape=(out, out, out), in_specs=[vmem] * 3, o...  0.84 us

profile of v4, /device:TPU:4, one launch (start us, length us, event | category | flops | bytes accessed | tf_op | source)
XLA Modules:
  0.0 12.4 jit_solution(3843882817081229989)
XLA Ops:
  1.3 10.3 %shard_map.175 = (f32[400,128]{1,0:T(8,128)S(1)}, f32[400,128]{1,0:T(8,128)S(1)}, f32[400,128]{1,0:T(8,128)S(1)}) custom-call(f32[400,128]{1,0:T(8,128)} %bitcast.9, f32[400,128]{1,0:T(8,128)} %bitcast.10, f32[400,128]{1,0:T(8,128)} %bitcast.11, f32[400,128]{1,0:T(8,128)} %bitcast.12, f32[400,128]{1,0:T(8,128)} %bitcast.13, f32[400,128]{1,0:T(8,128)} %bitcast.14, ...), custom_call_target="tpu_custom_call" | custom-call | tf_op jit(solution)/shard_map/pallas_call | solution.py:510
  11.6 0.8 %shard_map.176 = (f32[400,128]{1,0:T(8,128)}, f32[400,128]{1,0:T(8,128)}, f32[400,128]{1,0:T(8,128)}) custom-call(f32[400,128]{1,0:T(8,128)S(1)} %get-tuple-element.9.one, f32[400,128]{1,0:T(8,128)S(1)} %get-tuple-element.10.two, f32[400,128]{1,0:T(8,128)S(1)} %get-tuple-element.11.three), custom_call_target="tpu_custom_call" | custom-call | tf_op jit(solution)/shard_map/pallas_call | solution.py:568
